TPU v7x, 32 devices: a whole 2x2x4 slice. The times are simulated.
32 devices in a mesh: row: 4 (over y, core), col: 8 (over z, x).
Axes of the slice: x: 2, y: 2, z: 4, core: 2. Of those that a mesh axis runs over, the one named last changes fastest.
Arguments:
- sources: bfloat16 [4, 8, 4, 256, 256], P('row', 'col'), may hold values from -6 to 6
- history: bfloat16 [4, 8, 8, 256, 256], P(None, 'col'), may hold values from -4 to 4
- inverse_diagonal: float32 [4, 8, 256], P('row', 'col'), may hold values from 0.3 to 0.6
- far_cores: bfloat16 [4, 8, 32, 4, 8, 8, 32], P('row', None, None, None, 'col'), may hold values from -0.09375 to 0.09375
- target_basis: bfloat16 [4, 8, 256, 32], P('row', 'col'), may hold values from -1 to 1
- source_basis: bfloat16 [4, 8, 256, 32], P(None, 'col'), may hold values from -0.375 to 0.375
- near_blocks: bfloat16 [4, 8, 3, 256, 8, 256], P('row', 'col'), may hold values from -0.078125 to 0.078125
- near_tile: int32 [4, 8, 3], P('row', 'col'), may hold values from 0 to 3
- near_count: int32 [4, 8], P('row', 'col'), may hold values from 1 to 3, as said below
Outputs:
- new_steps: bfloat16 [4, 8, 4, 256, 256], P('row', 'col')
- energies: float32 [4, 256], replicated
Inputs may be any that keep to these rules, and one draw needn't show every extreme that they name: Only slots below near_count are used; in every draw some tile has all 3 slots live.
All inputs are finite; a program needn't handle non-finite values.
Results may differ from a plain program's by a relative error of at most 0.011.
Values may be sent and summed in bfloat16 or wider, within the bound.
A program may use at most 192 MiB of HBM per device.

v0:
```python
import jax
import jax.numpy as jnp
from jax import lax
from jax.sharding import PartitionSpec as P


def local(
    sources,
    history,
    inverse_diagonal,
    far_cores,
    target_basis,
    source_basis,
    near_blocks,
    near_tile,
    near_count,
):
    row_count = history.shape[0]
    col_count = far_cores.shape[1]
    rank_size = far_cores.shape[2]
    lag_count = history.shape[2]
    tile_size = history.shape[3]
    field_count = history.shape[4]
    step_count = sources.shape[2]
    panel_total = row_count * col_count * tile_size
    column_past = history[:, 0]
    basis = source_basis[:, 0]
    projected = jnp.einsum(
        "pta,pktx->pkax", basis, column_past, preferred_element_type=jnp.float32
    ).astype(jnp.bfloat16)
    core_matrix = far_cores.reshape(col_count * rank_size, row_count * lag_count * rank_size)
    own_basis = target_basis[0, 0]
    scaling = inverse_diagonal[0, 0][:, None]
    blocks_here = near_blocks[0, 0]
    tiles_here = near_tile[0, 0]
    live_count = near_count[0, 0]
    outputs = []
    energy_rows = []
    for moment in range(step_count):
        partial_value = jnp.dot(
            core_matrix,
            projected.reshape(row_count * lag_count * rank_size, field_count),
            preferred_element_type=jnp.float32,
        )

        def add_block(slot, total):
            source = lax.dynamic_index_in_dim(
                column_past, tiles_here[slot], 0, keepdims=False
            ).reshape(lag_count * tile_size, field_count)
            block = lax.dynamic_index_in_dim(blocks_here, slot, 0, keepdims=False).reshape(
                tile_size, lag_count * tile_size
            )
            return total + jnp.dot(block, source, preferred_element_type=jnp.float32)

        near = lax.fori_loop(
            0, live_count, add_block, jnp.zeros((tile_size, field_count), jnp.float32)
        )
        own_core = lax.psum_scatter(
            partial_value.astype(jnp.bfloat16), "col", scatter_dimension=0, tiled=True
        )
        far = jnp.dot(own_basis, own_core, preferred_element_type=jnp.float32)
        fresh = (scaling * (sources[0, 0, moment].astype(jnp.float32) - far - near)).astype(
            jnp.bfloat16
        )
        outputs.append(fresh)
        squares = jnp.sum(jnp.square(fresh.astype(jnp.float32)), axis=0) / panel_total
        energy_rows.append(lax.psum(squares, ("row", "col")))
        if moment + 1 < step_count:
            gathered = lax.all_gather(fresh[None], "row", axis=0, tiled=True)
            column_past = jnp.concatenate([gathered[:, None], column_past[:, :-1]], axis=1)
            fresh_proj = jnp.einsum(
                "pta,ptx->pax", basis, gathered, preferred_element_type=jnp.float32
            ).astype(jnp.bfloat16)
            projected = jnp.concatenate([fresh_proj[:, None], projected[:, :-1]], axis=1)
    energies = jnp.stack(energy_rows, axis=0)
    new_steps = jnp.stack(outputs, axis=0)[None, None]
    return (new_steps, energies)


def solution(mesh):
    placed = (
        P("row", "col", None, None, None),
        P(None, "col", None, None, None),
        P("row", "col", None),
        P("row", None, None, None, "col", None, None),
        P("row", "col", None, None),
        P(None, "col", None, None),
        P("row", "col", None, None, None, None),
        P("row", "col", None),
        P("row", "col"),
    )
    return jax.shard_map(
        local,
        mesh=mesh,
        in_specs=placed,
        out_specs=(P("row", "col", None, None, None), P()),
        check_vma=False,
    )
```

profile of v0, /device:TPU:0, one launch (start us, length us, event | category | flops | bytes accessed | tf_op | source)
XLA Modules:
  0.0 396.6 jit_solution(5392760271177488294)
XLA Ops:
  7.2 3.5 reshape.69
  10.8 3.2 convolution_convert_fusion
  15.2 2.6 copy.29
  17.9 9.8 %while.40 = (s32[]{:T(128)}, f32[256,256]{1,0:T(8,128)S(1)}, s32[]{:T(128)}, bf16[3,256,8,256]{3,1,2,0:T(8,128)(2,1)S(1)}, s32[3]{0:T(128)S(1)}, /*index=5*/bf16...) while((s32[]{:T(128)}, f32[256,256]{1,0:T(8,128)S(1)}, s32[]{:T(128)}, ...), condition=%wide.region_2.3_spmd, body=%wide.region_1.2_spmd.sunk | while | flops 268500992 | bytes 2621629 | solution.py:55
  27.7 4.2 %slice.41 = bf16[4,7,256,256]{3,2,1,0:T(8,128)(2,1)} slice(bf16[4,8,256,256]{3,2,1,0:T(8,128)(2,1)} %get-tuple-element.477), slice={[0:4], [0:7], [0:256], [0:256]} | slice | bytes 7340032 | tf_op jit(solution)/shard_map/slice | solution.py:70
  33.8 46.1 %reduce-scatter.13.cloned.1.call-done = bf16[32,256]{1,0:T(8,128)(2,1)} async-done(((bf16[256,256]{1,0:T(8,128)(2,1)}), bf16[32,256]{1,0:T(8,128)(2,1)}) %reduce-scatter.13.cloned.1.call-update) | async-done | bytes 16400
  82.3 7.1 %all-gather = bf16[1024,256]{1,0:T(8,128)(2,1)S(1)} all-gather(bf16[256,256]{1,0:T(8,128)(2,1)S(1)} %get-tuple-element.197), channel_id=2, replica_groups=mesh['row'=4,'col'=8] {'row'}, dimensions={0}, use_global_device_ids=true | all-gather | bytes 655360 | tf_op jit(solution)/shard_map/all_gather | solution.py:69
  89.4 4.5 %pad_maximum_fusion = bf16[4,8,256,256]{3,2,1,0:T(8,128)(2,1)} fusion(bf16[4,1,256,256]{3,2,1,0:T(8,128)(2,1)S(1)} %bitcast.237, bf16[4,7,256,256]{3,2,1,0:T(8,128)(2,1)} %slice.41), kind=kLoop, calls=%fused_computation.29 | loop fusion | flops 2097152 | bytes 8388608 | tf_op jit(solution)/shard_map/concatenate | solution.py:70
  94.0 10.8 %while.41 = (s32[]{:T(128)}, f32[256,256]{1,0:T(8,128)S(1)}, s32[]{:T(128)}, bf16[3,256,8,256]{3,1,2,0:T(8,128)(2,1)S(1)}, s32[3]{0:T(128)S(1)}, /*index=5*/bf16...) while((s32[]{:T(128)}, f32[256,256]{1,0:T(8,128)S(1)}, s32[]{:T(128)}, ...), condition=%wide.region_5.6_spmd, body=%wide.region_4.5_spmd.sunk | while | flops 268500992 | bytes 2621629 | solution.py:55
  107.6 2.0 fusion.43
  114.4 3.5 fusion.25
  117.9 58.8 %reduce-scatter.15.cloned.1.call-done = bf16[32,256]{1,0:T(8,128)(2,1)} async-done(((bf16[256,256]{1,0:T(8,128)(2,1)}), bf16[32,256]{1,0:T(8,128)(2,1)}) %reduce-scatter.15.cloned.1.call-update) | async-done | bytes 16400
  179.2 7.1 %all-gather.1 = bf16[1024,256]{1,0:T(8,128)(2,1)S(1)} all-gather(bf16[256,256]{1,0:T(8,128)(2,1)S(1)} %get-tuple-element.195), channel_id=3, replica_groups=mesh['row'=4,'col'=8] {'row'}, dimensions={0}, use_global_device_ids=true | all-gather | bytes 655360 | tf_op jit(solution)/shard_map/all_gather | solution.py:69
  186.3 4.5 %pad_maximum_fusion.1 = bf16[4,8,256,256]{3,2,1,0:T(8,128)(2,1)} fusion(bf16[4,1,256,256]{3,2,1,0:T(8,128)(2,1)S(1)} %bitcast.240, bf16[4,7,256,256]{3,2,1,0:T(8,128)(2,1)} %fusion.25), kind=kLoop, calls=%fused_computation.31 | loop fusion | flops 2097152 | bytes 8388608 | tf_op jit(solution)/shard_map/concatenate | solution.py:70
  190.9 10.7 %while.42 = (s32[]{:T(128)}, f32[256,256]{1,0:T(8,128)S(1)}, s32[]{:T(128)}, bf16[3,256,8,256]{3,1,2,0:T(8,128)(2,1)S(1)}, s32[3]{0:T(128)S(1)}, /*index=5*/bf16...) while((s32[]{:T(128)}, f32[256,256]{1,0:T(8,128)S(1)}, s32[]{:T(128)}, ...), condition=%wide.region_8.9_spmd, body=%wide.region_7.8_spmd.sunk | while | flops 268500992 | bytes 2621629 | solution.py:55
  203.9 2.0 fusion.44
  210.8 3.4 fusion.24
  214.2 59.0 %reduce-scatter.17.cloned.1.call-done = bf16[32,256]{1,0:T(8,128)(2,1)} async-done(((bf16[256,256]{1,0:T(8,128)(2,1)}), bf16[32,256]{1,0:T(8,128)(2,1)}) %reduce-scatter.17.cloned.1.call-update) | async-done | bytes 16400
  274.3 7.1 %all-gather.2 = bf16[1024,256]{1,0:T(8,128)(2,1)S(1)} all-gather(bf16[256,256]{1,0:T(8,128)(2,1)S(1)} %get-tuple-element.193), channel_id=4, replica_groups=mesh['row'=4,'col'=8] {'row'}, dimensions={0}, use_global_device_ids=true | all-gather | bytes 655360 | tf_op jit(solution)/shard_map/all_gather | solution.py:69
  285.8 4.5 %pad_maximum_fusion.2 = bf16[4,8,256,256]{3,2,1,0:T(8,128)(2,1)} fusion(bf16[4,7,256,256]{3,2,1,0:T(8,128)(2,1)} %fusion.24, bf16[4,1,256,256]{3,2,1,0:T(8,128)(2,1)} %bitcast.246), kind=kLoop, calls=%fused_computation.32 | loop fusion | flops 2097152 | bytes 8388608 | tf_op jit(solution)/shard_map/concatenate | solution.py:70
  290.3 10.4 %while.43 = (s32[]{:T(128)}, f32[256,256]{1,0:T(8,128)S(1)}, s32[]{:T(128)}, bf16[3,256,8,256]{3,1,2,0:T(8,128)(2,1)S(1)}, s32[3]{0:T(128)S(1)}, /*index=5*/bf16...) while((s32[]{:T(128)}, f32[256,256]{1,0:T(8,128)S(1)}, s32[]{:T(128)}, ...), condition=%wide.region_11.12_spmd, body=%wide.region_10.11_spmd.sunk | while | flops 268500992 | bytes 2621629 | solution.py:55
  300.7 45.5 %reduce-scatter.19.cloned.1.call-done = bf16[32,256]{1,0:T(8,128)(2,1)} async-done(((bf16[256,256]{1,0:T(8,128)(2,1)}), bf16[32,256]{1,0:T(8,128)(2,1)}) %reduce-scatter.19.cloned.1.call-update) | async-done | bytes 16400
  347.4 40.1 %all-reduce = (f32[1,256]{1,0:T(1,128)S(1)}, f32[1,256]{1,0:T(1,128)S(1)}, f32[1,256]{1,0:T(1,128)S(1)}, f32[1,256]{1,0:T(1,128)S(1)}) all-reduce(f32[1,256]{1,0:T(1,128)S(1)} %bitcast.261, f32[1,256]{1,0:T(1,128)S(1)} %bitcast.260, f32[1,256]{1,0:T(1,128)S(1)} %bitcast.259, ...), channel_id=1, replica_groups=mesh['row'=4,'col'=8] {'row','col'}, use_global_device_ids=true, to_apply=%region_19.20 | all-reduce | flops 1024 | bytes 8192 | tf_op jit(solution)/shard_map/psum | solution.py:67
  388.1 1.9 maximum_bitcast_fusion
  (90 shorter events, 48.2 us)
Async XLA Ops:
  7.2 3.6 copy-start
  7.2 72.7 %reduce-scatter.13.cloned.1.call-start = ((), (), s32[]{:S(2)}) async-start(), calls=%async_computation.4 | async-start | bytes 147456
  10.8 4.4 %copy-start.1 = (bf16[256,1024]{1,0:T(8,128)(2,1)}, bf16[256,1024]{1,0:T(8,128)(2,1)S(1)}, u32[]{:S(2)}) copy-start(bf16[256,1024]{1,0:T(8,128)(2,1)S(1)} %reshape.69) | copy-start | bytes 1572868
  14.0 1.2 copy-start.4
  14.0 3.9 copy-start.15
  15.2 161.6 %reduce-scatter.15.cloned.1.call-start = ((), (), s32[]{:S(2)}) async-start(), calls=%async_computation.5 | async-start | bytes 147456
  27.6 52.2 %copy-start.9 = (bf16[1,1,256,32]{2,3,1,0:T(8,128)(2,1)S(1)}, bf16[1,1,256,32]{2,3,1,0:T(8,128)(2,1)}, u32[]{:S(2)}) copy-start(bf16[1,1,256,32]{2,3,1,0:T(8,128)(2,1)} %param.21) | copy-start | bytes 49156
  27.7 52.2 %copy-start.10 = (f32[1,1,256]{2,1,0:T(1,128)S(1)}, f32[1,1,256]{2,1,0:T(1,128)}, u32[]{:S(2)}) copy-start(f32[1,1,256]{2,1,0:T(1,128)} %param.19) | copy-start | bytes 3076
  81.6 0.6 copy-start.6
  89.4 4.5 %copy-start.2 = (bf16[1024,256]{1,0:T(8,128)(2,1)}, bf16[1024,256]{1,0:T(8,128)(2,1)S(1)}, u32[]{:S(2)}) copy-start(bf16[1024,256]{1,0:T(8,128)(2,1)S(1)} %all-gather) | copy-start | bytes 1572868
  104.8 0.5 copy-start.16
  111.4 161.8 %reduce-scatter.17.cloned.1.call-start = ((), (), s32[]{:S(2)}) async-start(), calls=%async_computation.6 | async-start | bytes 147456
  114.4 62.3 %copy-start.11 = (f32[1,1,256]{2,1,0:T(1,128)S(1)}, f32[1,1,256]{2,1,0:T(1,128)}, u32[]{:S(2)}) copy-start(f32[1,1,256]{2,1,0:T(1,128)} %param.19) | copy-start | bytes 3076
  178.5 0.6 copy-start.7
  186.3 4.5 %copy-start.3 = (bf16[1024,256]{1,0:T(8,128)(2,1)}, bf16[1024,256]{1,0:T(8,128)(2,1)S(1)}, u32[]{:S(2)}) copy-start(bf16[1024,256]{1,0:T(8,128)(2,1)S(1)} %all-gather.1) | copy-start | bytes 1572868
  186.3 4.6 %copy-start.17 = (s32[3]{0:T(128)S(1)}, s32[3]{0:T(128)}, u32[]{:S(2)}) copy-start(s32[3]{0:T(128)} %copy-done.16) | copy-start | bytes 40
  207.7 138.5 %reduce-scatter.19.cloned.1.call-start = ((), (), s32[]{:S(2)}) async-start(), calls=%async_computation.7 | async-start | bytes 147456
  210.8 62.4 %copy-start.12 = (f32[1,1,256]{2,1,0:T(1,128)S(1)}, f32[1,1,256]{2,1,0:T(1,128)}, u32[]{:S(2)}) copy-start(f32[1,1,256]{2,1,0:T(1,128)} %param.19) | copy-start | bytes 3076
  274.3 7.2 %copy-start.8 = (bf16[256,256]{1,0:T(8,128)(2,1)}, bf16[256,256]{1,0:T(8,128)(2,1)S(1)}, u32[]{:S(2)}) copy-start(bf16[256,256]{1,0:T(8,128)(2,1)S(1)} %get-tuple-element.193) | copy-start | bytes 393220
  281.5 0.8 copy-start.5
  285.7 4.5 %copy-start.18 = (s32[3]{0:T(128)S(1)}, s32[3]{0:T(128)}, u32[]{:S(2)}) copy-start(s32[3]{0:T(128)} %copy-done.16) | copy-start | bytes 40
  290.2 57.1 %copy-start.13 = (f32[256]{0:T(256)S(1)}, f32[256]{0:T(256)}, u32[]{:S(2)}) copy-start(f32[256]{0:T(256)} %broadcast_multiply_fusion.3) | copy-start | bytes 3076
  290.3 57.1 %copy-start.14 = (f32[256]{0:T(256)S(1)}, f32[256]{0:T(256)}, u32[]{:S(2)}) copy-start(f32[256]{0:T(256)} %broadcast_multiply_fusion.2) | copy-start | bytes 3076
Sparse Core Ops, SparseCore 0:
  15.3 64.5 reduce-scatter.12
  111.5 65.2 reduce-scatter.14
  207.8 65.3 reduce-scatter.16
  285.9 60.2 reduce-scatter.18
where the time goes:
time: 399 us; the launch traced here: 397 us
  waiting for transfers between devices  209 us (52%)
  blocking collectives  61.6 us (15%)
  other arithmetic  32.2 us (8%)
  matrix products  30.9 us (8%)
  local copies, waits for them, and re-layouts  24.7 us (6%)
  loops' own time  23.4 us (6%)
  between operations  14 us (4%)
    unnamed x8, waiting for transfers between devices  209 us
    psum x1, blocking collectives, local(): energy_rows.append(lax.psum(squares, ('row', 'col')))  40.1 us
    another operation x4, loops' own time, local(): lax.fori_loop(0, live_count, add_block, jnp.zeros((tile_size, field_count...  23.4 us
    all_gather x3, blocking collectives, local(): gathered = lax.all_gather(fresh[None], 'row', axis=0, tiled=True)  21.4 us
    concatenate x5, other arithmetic, local(): jnp.concatenate([gathered[:, None], column_past[:, :-1]], axis=1)  20.4 us
    dot_general x8, matrix products, add_block(): return total + jnp.dot(block, source, preferred_element_type=jnp.float32)  13.4 us
    unnamed x43, local copies, waits for them, and re-layouts  10.1 us
  transfers between devices with their start and end apart: 4, of which 4 were waited for; matrix products, arithmetic and copies ran while one was open for 9% of the time, Pallas kernels for 0%

commit v1 on v0

v1 whole, which is shorter than its diff:
```python
import functools

import jax
import jax.numpy as jnp
from jax import lax
from jax.experimental import pallas as pl
from jax.experimental.pallas import tpu as pltpu
from jax.sharding import PartitionSpec as P

MESH = pl.DeviceIdType.MESH
F32 = jnp.float32
BF16 = jnp.bfloat16


def march(
    rows,
    cols,
    panel_total,
    tiles_ref,
    count_ref,
    basis_hbm,
    history_hbm,
    cores_hbm,
    near_hbm,
    target_hbm,
    scaling_hbm,
    sources_hbm,
    steps_ref,
    energy_ref,
    basis,
    history,
    cores,
    near_blocks,
    target,
    scaling_row,
    sources,
    scaling,
    past_proj,
    fresh_tiles,
    fresh_proj,
    core_out,
    core_in,
    near_sum,
    partial_sum,
    energy_own,
    energy_rows,
    energy_mid,
    energy_cols,
    load_sems,
    tile_send,
    tile_recv,
    pass_send,
    pass_recv,
    proj_send,
    proj_recv,
    core_send,
    core_recv,
    erow_send,
    erow_recv,
    ecol_send,
    ecol_recv,
):
    step_count = sources.shape[0]
    lag_count, _, rank, fields = past_proj.shape
    tile = history.shape[2]
    slot_count = near_blocks.shape[0]
    width = rows * rank
    my_row = lax.axis_index("row")
    my_col = lax.axis_index("col")
    partner = my_row + 1 - 2 * lax.rem(my_row, 2)

    def row_peer(d):
        return lax.rem(my_row + d, rows)

    def col_peer(d):
        return lax.rem(my_col + d, cols)

    loads = [
        pltpu.make_async_copy(src, dst, load_sems.at[n])
        for n, (src, dst) in enumerate(
            (
                (basis_hbm, basis),
                (history_hbm, history),
                (cores_hbm, cores),
                (near_hbm, near_blocks),
                (target_hbm, target),
                (scaling_hbm, scaling_row),
                (sources_hbm, sources),
            )
        )
    ]
    for load in loads:
        load.start()

    barrier = pltpu.get_barrier_semaphore()
    for d in range(1, rows):
        pl.semaphore_signal(barrier, inc=1, device_id={"row": row_peer(d)}, device_id_type=MESH)
    for d in range(1, cols):
        pl.semaphore_signal(barrier, inc=1, device_id={"col": col_peer(d)}, device_id_type=MESH)

    def row_copy(src, dst, send, recv, to):
        return pltpu.make_async_remote_copy(
            src_ref=src, dst_ref=dst, send_sem=send, recv_sem=recv,
            device_id={"row": to}, device_id_type=MESH,
        )

    def col_copy(src, dst, send, recv, to):
        return pltpu.make_async_remote_copy(
            src_ref=src, dst_ref=dst, send_sem=send, recv_sem=recv,
            device_id={"col": to}, device_id_type=MESH,
        )

    def proj_copy(n, owner, d):
        return row_copy(
            fresh_proj.at[n, owner], fresh_proj.at[n, owner],
            proj_send.at[n, d], proj_recv.at[n, owner], row_peer(d),
        )

    def tile_copy(n, owner, d):
        return row_copy(
            fresh_tiles[n].at[owner], fresh_tiles[n].at[owner],
            tile_send.at[n, d], tile_recv.at[n, owner], row_peer(d),
        )

    def pass_copy(n, owner):
        return row_copy(
            fresh_tiles[n].at[owner], fresh_tiles[n].at[owner],
            pass_send.at[n, owner], pass_recv.at[n, owner], partner,
        )

    def core_copy(n, d):
        to = col_peer(d)
        return col_copy(
            core_out.at[n, to], core_in.at[n, my_col],
            core_send.at[n, d], core_recv.at[n, my_col], to,
        )

    def core_arrival(n, origin):
        return col_copy(
            core_out.at[n, origin], core_in.at[n, origin],
            core_send.at[n, 0], core_recv.at[n, origin], origin,
        )

    def far_base(n):
        depth = lag_count - n
        total = jnp.dot(
            cores[:, n * width:],
            past_proj[0:depth].reshape(depth * width, fields),
            preferred_element_type=F32,
        )
        for lag in range(1, n):
            total += jnp.dot(
                cores[:, lag * width:(lag + 1) * width],
                fresh_proj[n - 1 - lag].reshape(width, fields),
                preferred_element_type=F32,
            )
        return total

    def near_base(n):
        depth = lag_count - n

        def add_slot(slot, carry):
            where = tiles_ref[slot]
            value = jnp.dot(
                near_blocks[slot, :, n * tile:],
                history[where, 0:depth].reshape(depth * tile, fields),
                preferred_element_type=F32,
            )
            for lag in range(1, n):
                value += jnp.dot(
                    near_blocks[slot, :, lag * tile:(lag + 1) * tile],
                    fresh_tiles[n - 1 - lag][where],
                    preferred_element_type=F32,
                )
            near_sum[n] += jnp.where(slot < count_ref[0], value, 0.0)
            return carry

        near_sum[n] = jnp.zeros((tile, fields), F32)
        lax.fori_loop(0, slot_count, add_slot, 0)

    def near_fresh(n):
        def add_slot(slot, carry):
            value = jnp.dot(
                near_blocks[slot, :, 0:tile],
                fresh_tiles[n - 1][tiles_ref[slot]],
                preferred_element_type=F32,
            )
            near_sum[n] += jnp.where(slot < count_ref[0], value, 0.0)
            return carry

        lax.fori_loop(0, slot_count, add_slot, 0)

    loads[0].wait()
    loads[1].wait()

    def project_lag(lag, carry):
        for p in range(rows):
            past_proj[lag, p] = jnp.dot(
                basis[p], history[p, lag], preferred_element_type=F32
            ).astype(BF16)
        return carry

    lax.fori_loop(0, lag_count, project_lag, 0)
    loads[2].wait()

    for n in range(step_count):
        if n == 0:
            partial = far_base(0)
        else:
            for d in range(1, rows):
                proj_copy(n - 1, row_peer(d), d).wait_recv()
            partial = partial_sum[...] + jnp.dot(
                cores[:, 0:width],
                fresh_proj[n - 1].reshape(width, fields),
                preferred_element_type=F32,
            )
        core_out[n] = partial.astype(BF16).reshape(cols, rank, fields)
        if n == 0:
            pl.semaphore_wait(barrier, rows - 1 + cols - 1)
        for d in range(1, cols):
            core_copy(n, d).start()
        if n == 0:
            loads[3].wait()
            near_base(0)
            loads[4].wait()
            loads[5].wait()
            loads[6].wait()
            scaling[...] = jnp.transpose(jnp.broadcast_to(scaling_row[...], (fields, tile)))
        else:
            for d in range(2, rows, 2):
                tile_copy(n - 1, row_peer(d), d).wait_recv()
                pass_copy(n - 1, row_peer(d)).start()
            tile_copy(n - 1, partner, 1).wait_recv()
            for d in range(2, rows, 2):
                pass_copy(n - 1, lax.rem(partner + d, rows)).wait_recv()
            near_fresh(n)
        core = core_out[n, my_col].astype(F32)
        for d in range(1, cols):
            origin = col_peer(d)
            core_arrival(n, origin).wait_recv()
            core += core_in[n, origin].astype(F32)
        far = lax.dot_general(
            target[...], core.astype(BF16), (((0,), (0,)), ((), ())),
            preferred_element_type=F32,
        )
        fresh = (scaling[...] * (sources[n].astype(F32) - far - near_sum[n])).astype(BF16)
        if n + 1 < step_count:
            fresh_tiles[n][my_row] = fresh
            row_copy(
                fresh_tiles[n].at[my_row], fresh_tiles[n].at[my_row],
                tile_send.at[n, 0], tile_recv.at[n, my_row], partner,
            ).start()
            fresh_proj[n, my_row] = jnp.dot(
                basis[my_row], fresh, preferred_element_type=F32
            ).astype(BF16)
            for d in range(1, rows):
                proj_copy(n, my_row, d).start()
            for d in range(2, rows, 2):
                tile_copy(n, my_row, d).start()
        steps_ref[n] = fresh
        energy_own[n:n + 1, :] = (
            jnp.sum(jnp.square(fresh.astype(F32)), axis=0, keepdims=True) / panel_total
        )
        if n + 1 < step_count:
            partial_sum[...] = far_base(n + 1)
            near_base(n + 1)

    def erow_copy(origin, d):
        return row_copy(
            energy_own, energy_rows.at[origin], erow_send.at[d], erow_recv.at[origin], row_peer(d)
        )

    def ecol_copy(origin, d):
        return col_copy(
            energy_mid, energy_cols.at[origin], ecol_send.at[d], ecol_recv.at[origin], col_peer(d)
        )

    for d in range(1, rows):
        erow_copy(my_row, d).start()
    energy_rows[my_row] = energy_own[...]
    for d in range(1, rows):
        erow_copy(row_peer(d), d).wait_recv()
    total = energy_rows[0]
    for p in range(1, rows):
        total += energy_rows[p]
    energy_mid[...] = total
    for d in range(1, cols):
        ecol_copy(my_col, d).start()
    energy_cols[my_col] = total
    for d in range(1, cols):
        ecol_copy(col_peer(d), d).wait_recv()
    total = energy_cols[0]
    for q in range(1, cols):
        total += energy_cols[q]
    energy_ref[...] = total

    for n in range(step_count):
        for d in range(1, cols):
            core_copy(n, d).wait_send()
        if n + 1 < step_count:
            row_copy(
                fresh_tiles[n].at[my_row], fresh_tiles[n].at[my_row],
                tile_send.at[n, 0], tile_recv.at[n, my_row], partner,
            ).wait_send()
            for d in range(1, rows):
                proj_copy(n, my_row, d).wait_send()
            for d in range(2, rows, 2):
                tile_copy(n, my_row, d).wait_send()
                pass_copy(n, row_peer(d)).wait_send()
    for d in range(1, rows):
        erow_copy(my_row, d).wait_send()
    for d in range(1, cols):
        ecol_copy(my_col, d).wait_send()


def local(
    sources,
    history,
    inverse_diagonal,
    far_cores,
    target_basis,
    source_basis,
    near_blocks,
    near_tile,
    near_count,
):
    rows, _, lags, tile, fields = history.shape
    cols, rank = far_cores.shape[1:3]
    steps = sources.shape[2]
    slots = near_blocks.shape[2]
    panel_total = rows * cols * tile
    cores = jnp.transpose(far_cores.reshape(cols * rank, rows, lags, rank), (0, 2, 1, 3)).reshape(
        cols * rank, lags * rows * rank
    )
    near = near_blocks.reshape(slots, tile, lags * tile)
    dma = pltpu.SemaphoreType.DMA
    anywhere = pl.BlockSpec(memory_space=pl.ANY)
    scalar = pl.BlockSpec(memory_space=pltpu.SMEM)
    inside = pl.BlockSpec(memory_space=pltpu.VMEM)
    new_steps, energies = pl.pallas_call(
        functools.partial(march, rows, cols, panel_total),
        out_shape=(
            jax.ShapeDtypeStruct((steps, tile, fields), BF16),
            jax.ShapeDtypeStruct((steps, fields), F32),
        ),
        in_specs=[scalar, scalar] + [anywhere] * 7,
        out_specs=(inside, inside),
        scratch_shapes=[
            pltpu.VMEM((rows, rank, tile), BF16),
            pltpu.VMEM((rows, lags, tile, fields), BF16),
            pltpu.VMEM((cols * rank, lags * rows * rank), BF16),
            pltpu.VMEM((slots, tile, lags * tile), BF16),
            pltpu.VMEM((rank, tile), BF16),
            pltpu.VMEM((1, tile), F32),
            pltpu.VMEM((steps, tile, fields), BF16),
            pltpu.VMEM((tile, fields), F32),
            pltpu.VMEM((lags, rows, rank, fields), BF16),
            tuple(pltpu.VMEM((rows, tile, fields), BF16) for _ in range(steps - 1)),
            pltpu.VMEM((steps - 1, rows, rank, fields), BF16),
            pltpu.VMEM((steps, cols, rank, fields), BF16),
            pltpu.VMEM((steps, cols, rank, fields), BF16),
            pltpu.VMEM((steps, tile, fields), F32),
            pltpu.VMEM((cols * rank, fields), F32),
            pltpu.VMEM((steps, fields), F32),
            pltpu.VMEM((rows, steps, fields), F32),
            pltpu.VMEM((steps, fields), F32),
            pltpu.VMEM((cols, steps, fields), F32),
            dma((7,)),
            dma((steps - 1, rows)),
            dma((steps - 1, rows)),
            dma((steps - 1, rows)),
            dma((steps - 1, rows)),
            dma((steps - 1, rows)),
            dma((steps - 1, rows)),
            dma((steps, cols)),
            dma((steps, cols)),
            dma((rows,)),
            dma((rows,)),
            dma((cols,)),
            dma((cols,)),
        ],
        compiler_params=pltpu.CompilerParams(
            collective_id=0, has_side_effects=True, vmem_limit_bytes=56 * 1024 * 1024
        ),
    )(
        near_tile.reshape(slots),
        near_count.reshape(1),
        jnp.swapaxes(source_basis[:, 0], 1, 2),
        history[:, 0],
        cores,
        near,
        jnp.swapaxes(target_basis[0, 0], 0, 1),
        inverse_diagonal[0],
        sources[0, 0],
    )
    return new_steps[None, None], energies


def solution(mesh):
    placed = (
        P("row", "col", None, None, None),
        P(None, "col", None, None, None),
        P("row", "col", None),
        P("row", None, None, None, "col", None, None),
        P("row", "col", None, None),
        P(None, "col", None, None),
        P("row", "col", None, None, None, None),
        P("row", "col", None),
        P("row", "col"),
    )
    return jax.shard_map(
        local,
        mesh=mesh,
        in_specs=placed,
        out_specs=(P("row", "col", None, None, None), P()),
        check_vma=False,
    )
```

time: 399 us -> 61.5 us (0.15)
  waiting for transfers between devices: 209 us -> 0 us
  blocking collectives: 61.6 us -> 0 us
  Pallas kernels: 0 us -> 47.7 us
  other arithmetic: 32.2 us -> 0 us
  matrix products: 30.9 us -> 0 us
  loops' own time: 23.4 us -> 0 us
  between operations: 14 us -> 1.44 us
  local copies, waits for them, and re-layouts: 24.7 us -> 12.2 us
    unnamed x8 -> x0, waiting for transfers between devices: 209 us -> none
    pallas_call x0 -> x1, Pallas kernels: none -> 47.7 us  [local(): pl.pallas_call(functools.partial(march, rows, cols, panel_total), out_sha...]
    psum x1 -> x0, blocking collectives: 40.1 us -> none  [local(): energy_rows.append(lax.psum(squares, ('row', 'col')))]
    dot_general x20 -> x0, matrix products: 30.9 us -> none  [the longest x8 13.4 us: add_block(): return total + jnp.dot(block, source, preferred_element_type=jnp.float32)]
    concatenate x10 -> x0, other arithmetic: 27.3 us -> none  [the longest x5 20.4 us: local(): jnp.concatenate([gathered[:, None], column_past[:, :-1]], axis=1)]
    another operation x4 -> x0, loops' own time: 23.4 us -> none  [local(): lax.fori_loop(0, live_count, add_block, jnp.zeros((tile_size, field_count...]
    all_gather x3 -> x0, blocking collectives: 21.4 us -> none  [local(): gathered = lax.all_gather(fresh[None], 'row', axis=0, tiled=True)]
    unnamed x43 -> x4, local copies, waits for them, and re-layouts: 10.1 us -> 3.14 us
  transfers between devices with their start and end apart: 4 -> 0, of which waited for: 4 -> 0; matrix products, arithmetic and copies ran while one was open for 9% -> 0% of each run, Pallas kernels for 0% -> 0%
where the time goes in v1:
time: 61.5 us; the launch traced here: 61.3 us
  Pallas kernels  47.7 us (78%)
  local copies, waits for them, and re-layouts  12.2 us (20%)
  between operations  1.44 us (2%)
    pallas_call x1, Pallas kernels, local(): pl.pallas_call(functools.partial(march, rows, cols, panel_total), out_sha...  47.7 us
    reshape x1, local copies, waits for them, and re-layouts, local(): far_cores.reshape(cols * rank, rows, lags, rank)  3.61 us
    reshape x1, local copies, waits for them, and re-layouts, local(): near = near_blocks.reshape(slots, tile, lags * tile)  3.37 us
    unnamed x4, local copies, waits for them, and re-layouts  3.14 us
    reshape x1, local copies, waits for them, and re-layouts, local(): jnp.transpose(far_cores.reshape(cols * rank, rows, lags, rank), (0, 2, 1,...  2.04 us

profile of v1, /device:TPU:0, one launch (start us, length us, event | category | flops | bytes accessed | tf_op | source)
XLA Modules:
  0.0 61.3 jit_solution(1097240486517030169)
XLA Ops:
  0.6 0.0 copy-start
  1.4 3.6 %copy.14 = bf16[256,4,8,32]{0,3,1,2:T(8,128)(2,1)} copy(bf16[256,4,8,32]{3,2,1,0:T(8,128)(2,1)} %bitcast.20) | data formatting | bytes 1048576 | tf_op jit(solution)/shard_map/reshape | solution.py:332
  5.0 2.0 %copy.13.cores_hbm = bf16[256,1024]{1,0:T(8,128)(2,1)} copy(bf16[256,1024]{0,1:T(8,128)(2,1)} %bitcast.21) | data formatting | bytes 1048576 | tf_op jit(solution)/shard_map/reshape | solution.py:332
  7.1 0.0 copy-done
  7.1 3.4 %reshape.23.near_hbm = bf16[3,256,2048]{2,1,0:T(8,128)(2,1)} reshape(bf16[1,1,3,256,8,256]{5,4,3,2,1,0:T(8,128)(2,1)S(1)} %copy-done) | data formatting | bytes 6291456 | tf_op jit(solution)/shard_map/reshape | solution.py:335
  10.5 47.7 %shard_map.104 = (bf16[4,256,256]{2,1,0:T(8,128)(2,1)}, f32[4,256]{1,0:T(4,128)}) custom-call(s32[3]{0:T(128)} %bitcast.27, s32[1]{0:T(128)} %bitcast.18.count_ref, bf16[4,32,256]{2,1,0:T(8,128)(2,1)} %bitcast.24, bf16[4,8,256,256]{3,2,1,0:T(8,128)(2,1)} %bitcast.19, bf16[256,1024]{1,0:T(8,128)(2,1)} %copy.13.cores_hbm, ...), custom_call_target="tpu_custom_call" | custom-call | tf_op jit(solution)/shard_map/pallas_call | solution.py:340
  58.2 1.9 %copy.18 = bf16[1,1,4,256,256]{4,3,2,1,0:T(8,128)(2,1)} copy(bf16[1,1,4,256,256]{4,3,2,1,0:T(8,128)(2,1)} %bitcast.23) | data formatting | bytes 1048576
  60.0 1.3 %copy.19 = f32[4,256]{1,0:T(4,128)} copy(f32[4,256]{1,0:T(4,128)} %get-tuple-element.9) | data formatting | bytes 8192
Async XLA Ops:
  0.6 6.5 %copy-start = (bf16[1,1,3,256,8,256]{5,4,3,2,1,0:T(8,128)(2,1)S(1)}, bf16[1,1,3,256,8,256]{5,4,3,2,1,0:T(8,128)(2,1)}, u32[]{:S(2)}) copy-start(bf16[1,1,3,256,8,256]{5,4,3,2,1,0:T(8,128)(2,1)} %param.15) | copy-start | bytes 9437188

commit v2 on v1

--- a/solution.py
+++ b/solution.py
@@ -35,6 +35,9 @@
     scaling_row,
     sources,
     scaling,
+    cores_raw,
+    near_raw,
+    stage,
     past_proj,
     fresh_tiles,
     fresh_proj,
@@ -47,6 +50,7 @@
     energy_mid,
     energy_cols,
     load_sems,
+    history_sems,
     tile_send,
     tile_recv,
     pass_send,
@@ -80,16 +84,25 @@
         for n, (src, dst) in enumerate(
             (
                 (basis_hbm, basis),
-                (history_hbm, history),
-                (cores_hbm, cores),
-                (near_hbm, near_blocks),
+                (cores_hbm, cores_raw),
+                (near_hbm, near_raw),
                 (target_hbm, target),
                 (scaling_hbm, scaling_row),
                 (sources_hbm, sources),
             )
         )
     ]
-    for load in loads:
+
+    def history_load(lag):
+        return pltpu.make_async_copy(
+            history_hbm.at[:, lag], history.at[:, lag], history_sems.at[lag]
+        )
+
+    loads[0].start()
+    loads[1].start()
+    for lag in range(lag_count):
+        history_load(lag).start()
+    for load in loads[2:]:
         load.start()
 
     barrier = pltpu.get_barrier_semaphore()
@@ -190,10 +203,52 @@
 
         lax.fori_loop(0, slot_count, add_slot, 0)
 
+    lanes = stage.shape[2]
+    block = stage.shape[1] // lag_count
+
+    def spread(value):
+        for c in range(value.shape[1] // lanes):
+            stage[c] = value[:, c * lanes:(c + 1) * lanes]
+
+    def pick(lag, c):
+        return stage[c, pl.ds(lag, block, stride=lag_count), :].astype(BF16)
+
+    def pack_cores(g, carry):
+        here = pl.ds(pl.multiple_of(g * block, block), block)
+        total = None
+        for p in range(rows):
+            value = cores_raw[here, p].astype(F32).reshape(block * lag_count, rank).astype(BF16)
+            place = (
+                lax.broadcasted_iota(jnp.int32, (rank, width), 1)
+                == lax.broadcasted_iota(jnp.int32, (rank, width), 0) + p * rank
+            )
+            term = jnp.dot(
+                value, place.astype(F32).astype(BF16), preferred_element_type=F32
+            )
+            total = term if total is None else total + term
+        spread(total)
+        for lag in range(lag_count):
+            for c in range(width // lanes):
+                first = lag * width + c * lanes
+                cores[here, first:first + lanes] = pick(lag, c)
+        return carry
+
+    def pack_near(index, carry):
+        slot = index // (tile // block)
+        here = pl.ds(pl.multiple_of(lax.rem(index, tile // block) * block, block), block)
+        spread(near_raw[slot, here].astype(F32).reshape(block * lag_count, tile))
+        for lag in range(lag_count):
+            for c in range(tile // lanes):
+                first = lag * tile + c * lanes
+                near_blocks[slot, here, first:first + lanes] = pick(lag, c)
+        return carry
+
+    loads[1].wait()
+    lax.fori_loop(0, cores.shape[0] // block, pack_cores, 0)
     loads[0].wait()
-    loads[1].wait()
 
     def project_lag(lag, carry):
+        history_load(lag).wait()
         for p in range(rows):
             past_proj[lag, p] = jnp.dot(
                 basis[p], history[p, lag], preferred_element_type=F32
@@ -201,7 +256,6 @@
         return carry
 
     lax.fori_loop(0, lag_count, project_lag, 0)
-    loads[2].wait()
 
     for n in range(step_count):
         if n == 0:
@@ -220,13 +274,14 @@
         for d in range(1, cols):
             core_copy(n, d).start()
         if n == 0:
-            loads[3].wait()
+            loads[2].wait()
+            lax.fori_loop(0, slot_count * (tile // block), pack_near, 0)
             near_base(0)
-            loads[4].wait()
-            loads[5].wait()
-            loads[6].wait()
+            for load in loads[3:]:
+                load.wait()
             scaling[...] = jnp.transpose(jnp.broadcast_to(scaling_row[...], (fields, tile)))
         else:
+            near_base(n)
             for d in range(2, rows, 2):
                 tile_copy(n - 1, row_peer(d), d).wait_recv()
                 pass_copy(n - 1, row_peer(d)).start()
@@ -263,7 +318,6 @@
         )
         if n + 1 < step_count:
             partial_sum[...] = far_base(n + 1)
-            near_base(n + 1)
 
     def erow_copy(origin, d):
         return row_copy(
@@ -313,6 +367,11 @@
         ecol_copy(my_col, d).wait_send()
 
 
+def hand_over(steps_in, energy_in, steps_out, energy_out):
+    steps_out[...] = steps_in[...]
+    energy_out[...] = energy_in[...]
+
+
 def local(
     sources,
     history,
@@ -329,12 +388,10 @@
     steps = sources.shape[2]
     slots = near_blocks.shape[2]
     panel_total = rows * cols * tile
-    cores = jnp.transpose(far_cores.reshape(cols * rank, rows, lags, rank), (0, 2, 1, 3)).reshape(
-        cols * rank, lags * rows * rank
-    )
-    near = near_blocks.reshape(slots, tile, lags * tile)
+    lanes = min(128, tile, rows * rank)
+    block = min(64, tile)
     dma = pltpu.SemaphoreType.DMA
-    anywhere = pl.BlockSpec(memory_space=pl.ANY)
+    anywhere = pl.BlockSpec(memory_space=pltpu.HBM)
     scalar = pl.BlockSpec(memory_space=pltpu.SMEM)
     inside = pl.BlockSpec(memory_space=pltpu.VMEM)
     new_steps, energies = pl.pallas_call(
@@ -354,6 +411,9 @@
             pltpu.VMEM((1, tile), F32),
             pltpu.VMEM((steps, tile, fields), BF16),
             pltpu.VMEM((tile, fields), F32),
+            pltpu.VMEM((cols * rank, rows, lags, rank), BF16),
+            pltpu.VMEM((slots, tile, lags, tile), BF16),
+            pltpu.VMEM((max(tile, rows * rank) // lanes, block * lags, lanes), F32),
             pltpu.VMEM((lags, rows, rank, fields), BF16),
             tuple(pltpu.VMEM((rows, tile, fields), BF16) for _ in range(steps - 1)),
             pltpu.VMEM((steps - 1, rows, rank, fields), BF16),
@@ -365,7 +425,8 @@
             pltpu.VMEM((rows, steps, fields), F32),
             pltpu.VMEM((steps, fields), F32),
             pltpu.VMEM((cols, steps, fields), F32),
-            dma((7,)),
+            dma((6,)),
+            dma((lags,)),
             dma((steps - 1, rows)),
             dma((steps - 1, rows)),
             dma((steps - 1, rows)),
@@ -380,19 +441,28 @@
             dma((cols,)),
         ],
         compiler_params=pltpu.CompilerParams(
-            collective_id=0, has_side_effects=True, vmem_limit_bytes=56 * 1024 * 1024
+            collective_id=0, has_side_effects=True, vmem_limit_bytes=58 * 1024 * 1024
         ),
     )(
         near_tile.reshape(slots),
         near_count.reshape(1),
         jnp.swapaxes(source_basis[:, 0], 1, 2),
         history[:, 0],
-        cores,
-        near,
+        far_cores.reshape(cols * rank, rows, lags, rank),
+        near_blocks[0, 0],
         jnp.swapaxes(target_basis[0, 0], 0, 1),
         inverse_diagonal[0],
         sources[0, 0],
     )
+    new_steps, energies = pl.pallas_call(
+        hand_over,
+        out_shape=(
+            jax.ShapeDtypeStruct((steps, tile, fields), BF16),
+            jax.ShapeDtypeStruct((steps, fields), F32),
+        ),
+        in_specs=(inside, inside),
+        out_specs=(inside, inside),
+    )(new_steps, energies)
     return new_steps[None, None], energies
 
 

time: 61.5 us -> 52.2 us (0.85)
  local copies, waits for them, and re-layouts: 12.2 us -> 0 us
  Pallas kernels: 47.7 us -> 50.8 us
    reshape x3 -> x0, local copies, waits for them, and re-layouts: 9.02 us -> none  [the longest x1 3.61 us: local(): far_cores.reshape(cols * rank, rows, lags, rank)]
    unnamed x4 -> x0, local copies, waits for them, and re-layouts: 3.14 us -> none
    pallas_call x0 -> x1, Pallas kernels: none -> 1.87 us  [local(): pl.pallas_call(hand_over, out_shape=(jax.ShapeDtypeStruct((steps, tile, f...]
    pallas_call x1, Pallas kernels: 47.7 us -> 48.9 us  [local(): pl.pallas_call(functools.partial(march, rows, cols, panel_total), out_sha...]
where the time goes in v2:
time: 52.2 us; the launch traced here: 52.1 us
  Pallas kernels  50.8 us (97%)
  between operations  1.29 us (2%)
    pallas_call x1, Pallas kernels, local(): pl.pallas_call(functools.partial(march, rows, cols, panel_total), out_sha...  48.9 us
    pallas_call x1, Pallas kernels, local(): pl.pallas_call(hand_over, out_shape=(jax.ShapeDtypeStruct((steps, tile, f...  1.87 us

profile of v2, /device:TPU:0, one launch (start us, length us, event | category | flops | bytes accessed | tf_op | source)
XLA Modules:
  0.0 52.1 jit_solution(16825386981706026939)
XLA Ops:
  1.3 48.9 %shard_map.104 = (bf16[4,256,256]{2,1,0:T(8,128)(2,1)}, f32[4,256]{1,0:T(4,128)}) custom-call(s32[3]{0:T(128)} %bitcast.22, s32[1]{0:T(128)} %bitcast.14.count_ref, bf16[4,32,256]{2,1,0:T(8,128)(2,1)} %bitcast.19, bf16[4,8,256,256]{3,2,1,0:T(8,128)(2,1)} %bitcast.15, bf16[256,4,8,32]{3,2,1,0:T(8,128)(2,1)} %bitcast.17, bf16[3,256,8,256]{3,2,1,0:T(8,128)(2,1)} %bitcast.16, ...), custom_call_target="tpu_custom_call" | custom-call | tf_op jit(solution)/shard_map/pallas_call | solution.py:397
  50.2 1.9 %shard_map.105 = (bf16[4,256,256]{2,1,0:T(8,128)(2,1)}, f32[4,256]{1,0:T(4,128)}) custom-call(bf16[4,256,256]{2,1,0:T(8,128)(2,1)} %get-tuple-element.6.steps_in, f32[4,256]{1,0:T(4,128)} %get-tuple-element.7.energy_in), custom_call_target="tpu_custom_call" | custom-call | tf_op jit(solution)/shard_map/pallas_call | solution.py:457

commit v3 on v2

--- a/solution.py
+++ b/solution.py
@@ -35,6 +35,7 @@
     scaling_row,
     sources,
     scaling,
+    last_tile,
     cores_raw,
     near_raw,
     stage,
@@ -51,6 +52,7 @@
     energy_cols,
     load_sems,
     history_sems,
+    result_sems,
     tile_send,
     tile_recv,
     pass_send,
@@ -154,6 +156,13 @@
             core_send.at[n, 0], core_recv.at[n, origin], origin,
         )
 
+    def result_copy(n):
+        return pltpu.make_async_copy(
+            fresh_tiles[n].at[my_row] if n + 1 < step_count else last_tile,
+            steps_ref.at[n],
+            result_sems.at[n],
+        )
+
     def far_base(n):
         depth = lag_count - n
         total = jnp.dot(
@@ -185,23 +194,21 @@
                     fresh_tiles[n - 1 - lag][where],
                     preferred_element_type=F32,
                 )
-            near_sum[n] += jnp.where(slot < count_ref[0], value, 0.0)
+            near_sum[n] += value
             return carry
 
         near_sum[n] = jnp.zeros((tile, fields), F32)
         lax.fori_loop(0, slot_count, add_slot, 0)
 
     def near_fresh(n):
-        def add_slot(slot, carry):
-            value = jnp.dot(
+        total = near_sum[n]
+        for slot in range(slot_count):
+            total += jnp.dot(
                 near_blocks[slot, :, 0:tile],
                 fresh_tiles[n - 1][tiles_ref[slot]],
                 preferred_element_type=F32,
             )
-            near_sum[n] += jnp.where(slot < count_ref[0], value, 0.0)
-            return carry
-
-        lax.fori_loop(0, slot_count, add_slot, 0)
+        near_sum[n] = sources[n].astype(F32) - total
 
     lanes = stage.shape[2]
     block = stage.shape[1] // lag_count
@@ -240,7 +247,9 @@
         for lag in range(lag_count):
             for c in range(tile // lanes):
                 first = lag * tile + c * lanes
-                near_blocks[slot, here, first:first + lanes] = pick(lag, c)
+                near_blocks[slot, here, first:first + lanes] = jnp.where(
+                    slot < count_ref[0], pick(lag, c), jnp.zeros((block, lanes), BF16)
+                )
         return carry
 
     loads[1].wait()
@@ -280,6 +289,7 @@
             for load in loads[3:]:
                 load.wait()
             scaling[...] = jnp.transpose(jnp.broadcast_to(scaling_row[...], (fields, tile)))
+            near_sum[0] = sources[0].astype(F32) - near_sum[0]
         else:
             near_base(n)
             for d in range(2, rows, 2):
@@ -298,7 +308,7 @@
             target[...], core.astype(BF16), (((0,), (0,)), ((), ())),
             preferred_element_type=F32,
         )
-        fresh = (scaling[...] * (sources[n].astype(F32) - far - near_sum[n])).astype(BF16)
+        fresh = (scaling[...] * (near_sum[n] - far)).astype(BF16)
         if n + 1 < step_count:
             fresh_tiles[n][my_row] = fresh
             row_copy(
@@ -312,7 +322,9 @@
                 proj_copy(n, my_row, d).start()
             for d in range(2, rows, 2):
                 tile_copy(n, my_row, d).start()
-        steps_ref[n] = fresh
+        else:
+            last_tile[...] = fresh
+        result_copy(n).start()
         energy_own[n:n + 1, :] = (
             jnp.sum(jnp.square(fresh.astype(F32)), axis=0, keepdims=True) / panel_total
         )
@@ -349,6 +361,7 @@
     energy_ref[...] = total
 
     for n in range(step_count):
+        result_copy(n).wait()
         for d in range(1, cols):
             core_copy(n, d).wait_send()
         if n + 1 < step_count:
@@ -401,7 +414,7 @@
             jax.ShapeDtypeStruct((steps, fields), F32),
         ),
         in_specs=[scalar, scalar] + [anywhere] * 7,
-        out_specs=(inside, inside),
+        out_specs=(anywhere, inside),
         scratch_shapes=[
             pltpu.VMEM((rows, rank, tile), BF16),
             pltpu.VMEM((rows, lags, tile, fields), BF16),
@@ -411,6 +424,7 @@
             pltpu.VMEM((1, tile), F32),
             pltpu.VMEM((steps, tile, fields), BF16),
             pltpu.VMEM((tile, fields), F32),
+            pltpu.VMEM((tile, fields), BF16),
             pltpu.VMEM((cols * rank, rows, lags, rank), BF16),
             pltpu.VMEM((slots, tile, lags, tile), BF16),
             pltpu.VMEM((max(tile, rows * rank) // lanes, block * lags, lanes), F32),
@@ -427,6 +441,7 @@
             pltpu.VMEM((cols, steps, fields), F32),
             dma((6,)),
             dma((lags,)),
+            dma((steps,)),
             dma((steps - 1, rows)),
             dma((steps - 1, rows)),
             dma((steps - 1, rows)),

time: 52.2 us -> 52.1 us (level)
  no operation moved by 1% of the time
where the time goes in v3:
time: 52.1 us; the launch traced here: 51.9 us
  Pallas kernels  50.6 us (97%)
  between operations  1.29 us (2%)
    pallas_call x1, Pallas kernels, local(): pl.pallas_call(functools.partial(march, rows, cols, panel_total), out_sha...  48.7 us
    pallas_call x1, Pallas kernels, local(): pl.pallas_call(hand_over, out_shape=(jax.ShapeDtypeStruct((steps, tile, f...  1.87 us

profile of v3, /device:TPU:0, one launch (start us, length us, event | category | flops | bytes accessed | tf_op | source)
XLA Modules:
  0.0 51.9 jit_solution(14783068041252925864)
XLA Ops:
  1.3 48.7 %shard_map.104 = (bf16[4,256,256]{2,1,0:T(8,128)(2,1)}, f32[4,256]{1,0:T(4,128)}) custom-call(s32[3]{0:T(128)} %bitcast.22, s32[1]{0:T(128)} %bitcast.14.count_ref, bf16[4,32,256]{2,1,0:T(8,128)(2,1)} %bitcast.19, bf16[4,8,256,256]{3,2,1,0:T(8,128)(2,1)} %bitcast.15, bf16[256,4,8,32]{3,2,1,0:T(8,128)(2,1)} %bitcast.17, bf16[3,256,8,256]{3,2,1,0:T(8,128)(2,1)} %bitcast.16, ...), custom_call_target="tpu_custom_call" | custom-call | tf_op jit(solution)/shard_map/pallas_call | solution.py:410
  50.0 1.9 %shard_map.105 = (bf16[4,256,256]{2,1,0:T(8,128)(2,1)}, f32[4,256]{1,0:T(4,128)}) custom-call(bf16[4,256,256]{2,1,0:T(8,128)(2,1)} %get-tuple-element.6.steps_in, f32[4,256]{1,0:T(4,128)} %get-tuple-element.7.energy_in), custom_call_target="tpu_custom_call" | custom-call | tf_op jit(solution)/shard_map/pallas_call | solution.py:472
